TPU v7x, 256 devices: a 2x2x32 block of a 4x8x32 slice. The times are simulated.
256 devices in a mesh: grp: 4 (over y, x), seq: 32 (over z), tp: 2 (over core).
Axes of the slice: x: 2, y: 2, z: 32, core: 2. Of those that a mesh axis runs over, the one named last changes fastest.
The devices are a block of a 4x8x32 slice.
Arguments:
- visual_q: bfloat16 [32768, 1536], P(('grp', 'seq'), 'tp'), parts along dimension 0, may hold values from -8 to 8
- visual_key_input: bfloat16 [32768, 1536], P(('grp', 'seq'), 'tp'), parts along dimension 0, may hold values from -8 to 8
- visual_v: bfloat16 [32768, 1536], P(('grp', 'seq'), 'tp'), parts along dimension 0, may hold values from -6 to 6
- text_k: bfloat16 [1024, 1536], P(('grp', 'seq'), 'tp'), parts along dimension 0, may hold values from -6 to 6
- text_v: bfloat16 [1024, 1536], P(('grp', 'seq'), 'tp'), parts along dimension 0, may hold values from -6 to 6
- text_mask: int32 [1024], P(('grp', 'seq')), parts along dimension 0, may hold values from 0 to 1, as said below
- slab_order: int32 [128], P(('grp', 'seq')), parts along dimension 0, may hold values from 0 to 31, each once
- q_gain: float32 [128], replicated, may hold values from 0.8 to 6
- key_norm_gain: float32 [128], replicated, may hold values from 0.8 to 6
- w_out: bfloat16 [1536, 3072], P('tp'), may hold values from -0.8984375 to 0.8984375
Outputs:
- attended: bfloat16 [32768, 3072], P(('grp', 'seq', 'tp')), parts along dimension 0
There are 4 independent parts, one for each index of `grp`. A program takes and returns all parts, laid end to end along the dimension named above; an argument that names none is the same for every part. Nothing has to cross between parts.
Inputs may be any that keep to these rules, and one draw needn't show every extreme that they name: `text_mask`: the first entries are 1 and the rest 0, with at least 32 ones. `slab_order`: each slab number once.
All inputs are finite; a program needn't handle non-finite values.
Results may differ from a plain program's by a relative error of at most 0.013.
The roundings to bfloat16 on the way count: a program that leaves them out, or rounds other values in their place, can miss the bound.
Values may be sent and summed in bfloat16 or wider, within the bound.
No kernel may reach another device: no remote copies, remote signals or barrier semaphores. Data moves between devices by JAX's collectives and lax.ppermute only.
A program may use at most 128 MiB of HBM per device.

v0:
```python
import jax
import jax.numpy as jnp
from jax import lax
from jax.sharding import PartitionSpec as P

PARTS = 4
SLAB_H = 2
WIDE = 32
PARTS = (32, 48, 48)
NEGATIVE = -1e30


def from_everyone(shard, axis):
    size = lax.axis_size(axis)
    return lax.all_to_all(
        jnp.broadcast_to(shard[None], (size, *shard.shape)), axis, 0, 0, tiled=True
    )


def of_everyone(shard, axis):
    return from_everyone(shard, axis).astype(jnp.float32).sum(axis=0)


def apply_norm(x, gain):
    x32 = x.astype(jnp.float32).reshape(x.shape[0], -1, 128)
    scale = lax.rsqrt(jnp.mean(x32 * x32, axis=-1, keepdims=True) + 0.05)
    return x32 * scale * gain


def angles(frame, height, column):
    pieces = []
    for pos, size in zip((frame, height, column), PARTS):
        half = size // 2
        freq = 10000.0 ** (-jnp.arange(half, dtype=jnp.float32) / half)
        pieces.append(pos.astype(jnp.float32)[:, None] * freq[None, :])
    angle = jnp.concatenate(pieces, axis=-1)
    return (jnp.cos(angle), jnp.sin(angle))


def apply_rotation(x, cosine_table, sine_table):
    outs = []
    offset = 0
    column = 0
    for size in PARTS:
        half = size // 2
        first = x[..., offset : offset + half]
        second = x[..., offset + half : offset + size]
        cpart = cosine_table[:, None, column : column + half]
        spart = sine_table[:, None, column : column + half]
        outs.append(first * cpart - second * spart)
        outs.append(second * cpart + first * spart)
        offset += size
        column += half
    return jnp.concatenate(outs, axis=-1)


def block_rows(count):
    for candidate in range(2048, 255, -1):
        if count % candidate == 0:
            return candidate
    return count


def absorb(carry, queries, key_rows, values, marks):
    count = key_rows.shape[0]
    heads = queries.shape[1]
    step_rows = block_rows(count)

    def update(state, block):
        key_block, value_block, mark_block = block
        top, total, accum = state
        scores = jnp.einsum(
            "qhd,khd->qhk",
            queries,
            key_block.reshape(-1, heads, 128),
            preferred_element_type=jnp.float32,
        )
        scores = scores + mark_block.astype(jnp.float32)[None, None, :]
        fresh_top = jnp.maximum(top, jnp.max(scores, axis=-1))
        probs = jnp.exp(scores - fresh_top[..., None])
        factor = jnp.exp(top - fresh_top)
        total = total * factor + jnp.sum(probs, axis=-1)
        mixed = jnp.einsum(
            "qhk,khd->qhd",
            probs.astype(jnp.bfloat16),
            value_block.reshape(-1, heads, 128),
            preferred_element_type=jnp.float32,
        )
        accum = accum * factor[..., None] + mixed
        return ((fresh_top, total, accum), None)

    if step_rows == count:
        return update(carry, (key_rows, values, marks))[0]
    turns = count // step_rows
    blocks = (
        key_rows.reshape(turns, step_rows, -1),
        values.reshape(turns, step_rows, -1),
        marks.reshape(turns, step_rows),
    )
    return lax.scan(update, carry, blocks)[0]


def body(
    visual_q,
    visual_key_input,
    visual_v,
    text_k,
    text_v,
    text_mask,
    slab_order,
    q_gain,
    key_norm_gain,
    w_out,
):
    rows = visual_q.shape[0]
    width = visual_q.shape[1]
    heads = width // 128
    local = jnp.arange(rows, dtype=jnp.int32)
    frame = local // (SLAB_H * WIDE)
    height = slab_order[0] * SLAB_H + local // WIDE % SLAB_H
    column = local % WIDE
    cosine_table, sine_table = angles(frame, height, column)
    queries = (
        apply_rotation(apply_norm(visual_q, q_gain), cosine_table, sine_table)
        / jnp.sqrt(jnp.float32(128))
    ).astype(jnp.bfloat16)
    visual_key_rows = (
        apply_rotation(apply_norm(visual_key_input, key_norm_gain), cosine_table, sine_table)
        .astype(jnp.bfloat16)
        .reshape(rows, width)
    )
    textual_keys = (
        apply_norm(text_k, key_norm_gain).astype(jnp.bfloat16).reshape(text_k.shape[0], width)
    )
    text_marks = jnp.where(text_mask == 1, 0.0, NEGATIVE).astype(jnp.bfloat16)
    start_state = (
        jnp.full((rows, heads), NEGATIVE, jnp.float32),
        jnp.zeros((rows, heads), jnp.float32),
        jnp.zeros((rows, heads, 128), jnp.float32),
    )
    joint_keys = jnp.concatenate([visual_key_rows, textual_keys], axis=0)
    joint_values = jnp.concatenate([visual_v, text_v], axis=0)
    joint_marks = jnp.concatenate([jnp.zeros((rows,), jnp.bfloat16), text_marks], axis=0)
    state = absorb(
        start_state,
        queries,
        lax.all_gather(joint_keys, "seq", axis=0, tiled=True),
        lax.all_gather(joint_values, "seq", axis=0, tiled=True),
        lax.all_gather(joint_marks, "seq", axis=0, tiled=True),
    )
    top, total, accum = state
    heads_out = (accum / total[..., None]).astype(jnp.bfloat16).reshape(rows, width)
    share = rows // lax.axis_size("tp")
    summed = of_everyone(
        jnp.dot(heads_out, w_out, preferred_element_type=jnp.float32).astype(jnp.bfloat16), "tp"
    ).astype(jnp.float32)
    kept = lax.dynamic_slice_in_dim(summed, lax.axis_index("tp") * share, share, 0)
    return kept.astype(jnp.bfloat16)


def solution(mesh):
    placed = (
        P(("grp", "seq"), "tp"),
        P(("grp", "seq"), "tp"),
        P(("grp", "seq"), "tp"),
        P(("grp", "seq"), "tp"),
        P(("grp", "seq"), "tp"),
        P(("grp", "seq")),
        P(("grp", "seq")),
        P(),
        P(),
        P("tp", None),
    )
    return jax.shard_map(
        body, mesh=mesh, in_specs=placed, out_specs=P(("grp", "seq", "tp"), None), check_vma=False
    )
```

profile of v0, /device:TPU:37, one launch (start us, length us, event | category | flops | bytes accessed | tf_op | source)
XLA Modules:
  0.0 474.0 jit_solution(3188589150645841553)
XLA Ops:
  7.4 0.1 broadcast_multiply_fusion.2
  7.5 0.1 broadcast_multiply_fusion.1
  7.5 0.2 fusion.25
  7.8 0.8 fusion.27
  8.6 0.7 broadcast_bitcast_fusion
  9.3 0.8 fusion.29
  10.1 0.2 copy.50
  10.3 1.2 copy.49
  11.4 0.1 fusion.14
  11.5 0.8 fusion.15
  12.6 1.0 copy.51
  13.7 0.8 pad_maximum_fusion.1
  14.6 0.7 dynamic-slice
  16.1 0.3 dynamic-update-slice
  16.3 113.2 %all-reduce.1 = bf16[8448]{0:T(1024)(128)(2,1)S(1)} all-reduce(bf16[8448]{0:T(1024)(128)(2,1)S(1)} %dynamic-update-slice), channel_id=1, replica_groups=mesh['grp'=4,'seq'=32,'tp'=2] {'seq'}, use_global_device_ids=true, to_apply=%add.1 | all-reduce | flops 8448 | bytes 33792
  129.6 0.2 copy.52
  129.8 0.1 fusion.16
  129.9 0.1 fusion.17
  130.2 0.1 multiply_convert_fusion
  130.3 0.2 copy.54
  130.5 58.8 %all-gather.3.cloned.1.call-done = bf16[8448,768]{1,0:T(8,128)(2,1)} async-done(((bf16[264,768]{1,0:T(8,128)(2,1)}), bf16[8448,768]{1,0:T(8,128)(2,1)}) %all-gather.3.cloned.1.call-update) | async-done | bytes 12976144 | tf_op jit(solution)/shard_map/all_gather | solution.py:147
  189.3 162.7 %all-gather.5.cloned.1.call-done = bf16[8448,768]{1,0:T(8,128)(2,1)} async-done(((bf16[264,768]{1,0:T(8,128)(2,1)}), bf16[8448,768]{1,0:T(8,128)(2,1)}) %all-gather.5.cloned.1.call-update) | async-done | bytes 12976144 | tf_op jit(solution)/shard_map/all_gather | solution.py:148
  352.0 98.3 %while.15 = (s32[]{:T(128)}, f32[256,6]{0,1:T(8,128)S(1)}, f32[256,6]{0,1:T(8,128)S(1)}, f32[256,6,128]{0,2,1:T(8,128)S(1)}, bf16[6,1408,768]{2,1,0:T(8,128)(2,1...) while((s32[]{:T(128)}, f32[256,6]{0,1:T(8,128)S(1)}, ...), condition=%wide.region_6.7_spmd.clone, body=%wide.region_3.6_spmd.clone.sunk | while | flops 1125196672 | bytes 49668988 | solution.py:100
  352.0 3.9 constant_dynamic-slice_fusion.3
  355.9 2.4 copy.62
  358.4 2.9 copy.63
  361.3 3.1 bitcast_reduce_fusion.2
  364.5 1.9 fusion.56
  366.3 2.0 fusion.58
  368.4 3.9 constant_dynamic-slice_fusion.3
  372.3 2.4 copy.62
  374.8 2.9 copy.63
  377.7 3.1 bitcast_reduce_fusion.2
  380.8 1.9 fusion.56
  382.7 2.0 fusion.58
  384.8 3.9 constant_dynamic-slice_fusion.3
  388.7 2.4 copy.62
  391.1 2.9 copy.63
  394.1 3.1 bitcast_reduce_fusion.2
  397.2 1.9 fusion.56
  399.1 2.0 fusion.58
  401.2 3.9 constant_dynamic-slice_fusion.3
  405.1 2.4 copy.62
  407.5 2.9 copy.63
  410.4 3.1 bitcast_reduce_fusion.2
  413.6 1.9 fusion.56
  415.5 2.0 fusion.58
  417.6 3.9 constant_dynamic-slice_fusion.3
  421.5 2.4 copy.62
  423.9 2.9 copy.63
  426.8 3.1 bitcast_reduce_fusion.2
  430.0 1.9 fusion.56
  431.9 2.0 fusion.58
  433.9 3.9 constant_dynamic-slice_fusion.3
  437.8 2.4 copy.62
  440.3 2.9 copy.63
  443.2 3.1 bitcast_reduce_fusion.2
  446.4 1.9 fusion.56
  448.2 2.0 fusion.58
  450.4 3.8 convolution_convert_fusion
  454.1 0.4 broadcast_in_dim.19
  454.5 11.1 %all_to_all.5 = bf16[2,256,3072]{2,1,0:T(8,128)(2,1)S(1)} all-to-all(bf16[2,256,3072]{2,1,0:T(8,128)(2,1)S(1)} %broadcast_in_dim.19), channel_id=1, replica_groups=mesh['grp'=4,'seq'=32,'tp'=2] {'tp'}, dimensions={0} | all-to-all | bytes 6291456 | tf_op jit(solution)/shard_map/all_to_all | solution.py:15
  465.6 0.6 convert_reduce_fusion.1
  466.2 0.9 dynamic-slice_convert_fusion
  (72 shorter events, 1.1 us)
Async XLA Ops:
  6.5 8.1 %copy-start.5 = (u32[256]{0:T(256)S(1)}, u32[256]{0:T(256)}, u32[]{:S(2)}) copy-start(u32[256]{0:T(256)} %constant.118) | copy-start | bytes 3076
  6.5 7.2 %copy-start.2 = (bf16[8,768]{1,0:T(8,128)(2,1)S(1)}, bf16[8,768]{1,0:T(8,128)(2,1)}, u32[]{:S(2)}) copy-start(bf16[8,768]{1,0:T(8,128)(2,1)} %param.16) | copy-start | bytes 36868
  6.6 7.2 %copy-start = (bf16[256,768]{1,0:T(8,128)(2,1)S(1)}, bf16[256,768]{1,0:T(8,128)(2,1)}, u32[]{:S(2)}) copy-start(bf16[256,768]{1,0:T(8,128)(2,1)} %param.14) | copy-start | bytes 1179652
  6.6 9.5 %copy-start.4 = (s32[8]{0:T(128)S(1)}, s32[8]{0:T(128)}, u32[]{:S(2)}) copy-start(s32[8]{0:T(128)} %param.17) | copy-start | bytes 100
  6.6 123.0 %copy-start.1 = (bf16[256,768]{1,0:T(8,128)(2,1)S(1)}, bf16[256,768]{1,0:T(8,128)(2,1)}, u32[]{:S(2)}) copy-start(bf16[256,768]{1,0:T(8,128)(2,1)} %param.12) | copy-start | bytes 1179652
  6.6 182.8 %all-gather.3.cloned.1.call-start = ((), (), s32[]{:S(2)}) async-start(), calls=%async_computation.1 | async-start | bytes 13381632 | tf_op jit(solution)/shard_map/all_gather | solution.py:147
  10.2 119.6 %copy-start.3 = (f32[128]{0:T(128)S(1)}, f32[128]{0:T(128)}, u32[]{:S(2)}) copy-start(f32[128]{0:T(128)} %param.19) | copy-start | bytes 1540
  13.6 338.4 %all-gather.5.cloned.1.call-start = ((), (), s32[]{:S(2)}) async-start(), calls=%async_computation.2 | async-start | bytes 13381632 | tf_op jit(solution)/shard_map/all_gather | solution.py:148
Sparse Core Ops, SparseCore 0:
  13.7 175.5 all-gather.2
  191.1 160.8 all-gather.4
where the time goes:
time: 475 us; the launch traced here: 474 us
  waiting for transfers between devices  222 us (47%)
  blocking collectives  124 us (26%)
  local copies, waits for them, and re-layouts  61.2 us (13%)
  matrix products  34.7 us (7%)
  other arithmetic  16.4 us (3%)
  between operations  15.2 us (3%)
    all_gather x1, waiting for transfers between devices, body(): lax.all_gather(joint_values, 'seq', axis=0, tiled=True)  163 us
    unnamed x1, blocking collectives  113 us
    all_gather x1, waiting for transfers between devices, body(): lax.all_gather(joint_keys, 'seq', axis=0, tiled=True)  58.8 us
    dynamic_slice x18, local copies, waits for them, and re-layouts, absorb(): return lax.scan(update, carry, blocks)[0]  55.4 us
    dot_general x6, matrix products, update(): jnp.einsum('qhd,khd->qhk', queries, key_block.reshape(-1, heads, 128), pr...  18.8 us
    dot_general x6, matrix products, update(): jnp.einsum('qhk,khd->qhd', probs.astype(jnp.bfloat16), value_block.reshap...  12.1 us
    reduce_sum x6, other arithmetic, update(): total = total * factor + jnp.sum(probs, axis=-1)  11.1 us
    all_to_all x1, blocking collectives, from_everyone(): lax.all_to_all(jnp.broadcast_to(shard[None], (size, *shard.shape)), axis,...  11.1 us
  transfers between devices with their start and end apart: 2, of which 2 were waited for; matrix products, arithmetic and copies ran while one was open for 1% of the time, Pallas kernels for 0%

commit v1 on v0

--- a/solution.py
+++ b/solution.py
@@ -8,6 +8,18 @@
 WIDE = 32
 PARTS = (32, 48, 48)
 NEGATIVE = -1e30
+
+
+def start_trees_over_axis(xx):
+    n = lax.axis_size("seq")
+    everything = lax.all_to_all(
+        jnp.tile(xx, tuple((n if tick == 0 else 1 for tick in range(xx.ndim)))),
+        "seq",
+        split_axis=0,
+        concat_axis=0,
+        tiled=True,
+    )
+    return everything
 
 
 def from_everyone(shard, axis):
@@ -145,7 +157,7 @@
         start_state,
         queries,
         lax.all_gather(joint_keys, "seq", axis=0, tiled=True),
-        lax.all_gather(joint_values, "seq", axis=0, tiled=True),
+        start_trees_over_axis(joint_values),
         lax.all_gather(joint_marks, "seq", axis=0, tiled=True),
     )
     top, total, accum = state

time: 475 us -> 1510 us (3.18)
  blocking collectives: 124 us -> 1340 us
  waiting for transfers between devices: 222 us -> 0.08 us
  starting transfers between devices: 0.13 us -> 33.4 us
    unnamed x1, blocking collectives: 113 us -> 1310 us
    all_gather x1 -> x0, waiting for transfers between devices: 163 us -> none  [body(): lax.all_gather(joint_values, 'seq', axis=0, tiled=True)]
    all_gather x1, waiting for transfers between devices: 58.8 us -> 0.02 us  [body(): lax.all_gather(joint_keys, 'seq', axis=0, tiled=True)]
    all_to_all x0 -> x1, starting transfers between devices: none -> 33.3 us  [start_trees_over_axis(): lax.all_to_all(jnp.tile(xx, tuple((n if tick == 0 else 1 for tick in rang...]
    all_to_all x1, blocking collectives: 11.1 us -> 30.4 us  [from_everyone(): lax.all_to_all(jnp.broadcast_to(shard[None], (size, *shard.shape)), axis,...]
  transfers between devices with their start and end apart: 2 -> 2, of which waited for: 2 -> 0; matrix products, arithmetic and copies ran while one was open for 1% -> 0% of each run, Pallas kernels for 0% -> 0%
where the time goes in v1:
time: 1510 us
  blocking collectives  1340 us (89%)
  local copies, waits for them, and re-layouts  65.1 us (4%)
  matrix products  34.7 us (2%)
  starting transfers between devices  33.4 us (2%)
  between operations  15.2 us (1%)
    unnamed x1, blocking collectives  1310 us
    dynamic_slice x18, local copies, waits for them, and re-layouts, absorb(): return lax.scan(update, carry, blocks)[0]  55.4 us
    all_to_all x1, starting transfers between devices, start_trees_over_axis(): lax.all_to_all(jnp.tile(xx, tuple((n if tick == 0 else 1 for tick in rang...  33.3 us
    all_to_all x1, blocking collectives, from_everyone(): lax.all_to_all(jnp.broadcast_to(shard[None], (size, *shard.shape)), axis,...  30.4 us
  transfers between devices with their start and end apart: 2, of which 0 were waited for; matrix products, arithmetic and copies ran while one was open for 0% of the time, Pallas kernels for 0%

profile of v1, /device:TPU:37, one launch (start us, length us, event | category | flops | bytes accessed | tf_op | source)
XLA Modules:
  0.0 1505.6 jit_solution(4993421953843216129)
XLA Ops:
  6.5 1.0 pad_maximum_fusion.1
  7.6 5.5 tile.2
  13.1 33.3 %all-to-all-start = ((bf16[32,264,768]{2,1,0:T(8,128)(2,1)}), bf16[32,264,768]{2,1,0:T(8,128)(2,1)}, u32[]{:S(2)}, u32[]{:S(2)}) async-start(bf16[32,264,768]{2,1,0:T(8,128)(2,1)} %tile.2), calls=%async_computation | async-start | bytes 25952256 | tf_op jit(solution)/shard_map/all_to_all | solution.py:15
  47.4 0.1 broadcast_multiply_fusion.2
  47.4 0.1 broadcast_multiply_fusion.1
  47.5 0.2 fusion.25
  47.8 0.1 fusion.27
  47.9 0.1 fusion.29
  48.0 0.2 copy.50
  48.2 0.2 copy.49
  48.3 0.1 fusion.14
  48.5 0.1 fusion.15
  48.9 1.0 copy.51
  50.0 0.7 dynamic-slice
  51.4 0.3 dynamic-update-slice
  51.6 1311.7 %all-reduce.1 = bf16[8448]{0:T(1024)(128)(2,1)S(1)} all-reduce(bf16[8448]{0:T(1024)(128)(2,1)S(1)} %dynamic-update-slice), channel_id=1, replica_groups=mesh['grp'=4,'seq'=32,'tp'=2] {'seq'}, use_global_device_ids=true, to_apply=%add.1 | all-reduce | flops 8448 | bytes 33792
  1363.4 0.2 copy.52
  1363.5 0.1 fusion.16
  1363.7 0.1 fusion.17
  1364.0 0.1 multiply_convert_fusion
  1364.0 0.2 copy.54
  1364.3 98.3 %while.15 = (s32[]{:T(128)}, f32[256,6]{0,1:T(8,128)S(1)}, f32[256,6]{0,1:T(8,128)S(1)}, f32[256,6,128]{0,2,1:T(8,128)S(1)}, bf16[6,1408,768]{2,1,0:T(8,128)(2,1...) while((s32[]{:T(128)}, f32[256,6]{0,1:T(8,128)S(1)}, ...), condition=%wide.region_6.7_spmd.clone, body=%wide.region_3.6_spmd.clone.sunk | while | flops 1125196672 | bytes 49668988 | solution.py:112
  1364.4 3.9 constant_dynamic-slice_fusion.3
  1368.3 2.4 copy.62
  1370.7 2.9 copy.63
  1373.6 3.1 bitcast_reduce_fusion.2
  1376.8 1.9 fusion.56
  1378.7 2.0 fusion.58
  1380.7 3.9 constant_dynamic-slice_fusion.3
  1384.6 2.4 copy.62
  1387.1 2.9 copy.63
  1390.0 3.1 bitcast_reduce_fusion.2
  1393.2 1.9 fusion.56
  1395.0 2.0 fusion.58
  1397.1 3.9 constant_dynamic-slice_fusion.3
  1401.0 2.4 copy.62
  1403.5 2.9 copy.63
  1406.4 3.1 bitcast_reduce_fusion.2
  1409.5 1.9 fusion.56
  1411.4 2.0 fusion.58
  1413.5 3.9 constant_dynamic-slice_fusion.3
  1417.4 2.4 copy.62
  1419.8 2.9 copy.63
  1422.8 3.1 bitcast_reduce_fusion.2
  1425.9 1.9 fusion.56
  1427.8 2.0 fusion.58
  1429.9 3.9 constant_dynamic-slice_fusion.3
  1433.8 2.4 copy.62
  1436.2 2.9 copy.63
  1439.1 3.1 bitcast_reduce_fusion.2
  1442.3 1.9 fusion.56
  1444.2 2.0 fusion.58
  1446.3 3.9 constant_dynamic-slice_fusion.3
  1450.2 2.4 copy.62
  1452.6 2.9 copy.63
  1455.5 3.1 bitcast_reduce_fusion.2
  1458.7 1.9 fusion.56
  1460.6 2.0 fusion.58
  1462.6 0.1 divide_convert_fusion
  1462.7 3.8 convolution_convert_fusion
  1466.4 0.4 broadcast_in_dim.19
  1466.8 30.4 %all_to_all.11 = bf16[2,256,3072]{2,1,0:T(8,128)(2,1)S(1)} all-to-all(bf16[2,256,3072]{2,1,0:T(8,128)(2,1)S(1)} %broadcast_in_dim.19), channel_id=1, replica_groups=mesh['grp'=4,'seq'=32,'tp'=2] {'tp'}, dimensions={0} | all-to-all | bytes 6291456 | tf_op jit(solution)/shard_map/all_to_all | solution.py:27
  1497.3 0.6 convert_reduce_fusion.1
  1497.8 0.9 dynamic-slice_convert_fusion
  (74 shorter events, 1.0 us)
Async XLA Ops:
  13.1 34.7 %copy-start.2 = (bf16[8,768]{1,0:T(8,128)(2,1)S(1)}, bf16[8,768]{1,0:T(8,128)(2,1)}, u32[]{:S(2)}) copy-start(bf16[8,768]{1,0:T(8,128)(2,1)} %param.15) | copy-start | bytes 36868
  13.1 34.7 %copy-start.3 = (f32[128]{0:T(128)S(1)}, f32[128]{0:T(128)}, u32[]{:S(2)}) copy-start(f32[128]{0:T(128)} %param.20) | copy-start | bytes 1540
  13.1 35.0 %copy-start = (bf16[256,768]{1,0:T(8,128)(2,1)S(1)}, bf16[256,768]{1,0:T(8,128)(2,1)}, u32[]{:S(2)}) copy-start(bf16[256,768]{1,0:T(8,128)(2,1)} %param.13) | copy-start | bytes 1179652
  13.1 1351.2 %all-to-all-start = ((bf16[32,264,768]{2,1,0:T(8,128)(2,1)}), bf16[32,264,768]{2,1,0:T(8,128)(2,1)}, u32[]{:S(2)}, u32[]{:S(2)}) async-start(bf16[32,264,768]{2,1,0:T(8,128)(2,1)} %tile.2), calls=%async_computation | async-start | bytes 25952256 | tf_op jit(solution)/shard_map/all_to_all | solution.py:15
  46.5 3.4 copy-start.6
  46.5 4.8 copy-start.5
  46.5 1316.8 %copy-start.1 = (bf16[256,768]{1,0:T(8,128)(2,1)S(1)}, bf16[256,768]{1,0:T(8,128)(2,1)}, u32[]{:S(2)}) copy-start(bf16[256,768]{1,0:T(8,128)(2,1)} %param.12) | copy-start | bytes 1179652
  46.5 1317.1 %copy-start.4 = (f32[128]{0:T(128)S(1)}, f32[128]{0:T(128)}, u32[]{:S(2)}) copy-start(f32[128]{0:T(128)} %param.19) | copy-start | bytes 1540
  46.5 1317.7 %all-gather.2.cloned.1.call-start = ((), (), s32[]{:S(2)}) async-start(), calls=%async_computation.2 | async-start | bytes 13381632 | tf_op jit(solution)/shard_map/all_gather | solution.py:159
Sparse Core Ops, SparseCore 0:
  50.0 1249.1 all-gather.1
